TPU v7x, 32 devices: a whole 2x2x4 slice. The times are simulated.
32 devices in a mesh: group: 2 (over x), tile: 16 (over z, y, core).
Axes of the slice: x: 2, y: 2, z: 4, core: 2. Of those that a mesh axis runs over, the one named last changes fastest.
Arguments:
- latents: bfloat16 [384, 16, 128], P(('group', 'tile')), parts along dimension 0, may hold values from -6 to 6
- clip_index: int32 [8], P('group'), parts along dimension 0, may hold values from 0 to 1, never falling along the last dimension, each value on 1 to 3 neighbouring positions
- first_conv: bfloat16 [3, 3, 3, 16, 384], replicated, may hold values from -0.3125 to 0.3125
- first_gain: float32 [384], replicated, may hold values from 0.4 to 1.6
- middle_conv: bfloat16 [3, 3, 3, 384, 384], replicated, may hold values from -0.0625 to 0.0625
- head_gain: float32 [384], replicated, may hold values from 0.4 to 1.6
- head_weight: bfloat16 [384, 48], replicated, may hold values from -0.3125 to 0.3125
Outputs:
- pixels: float32 [32, 2, 3, 48, 128], P(('group', 'tile')), parts along dimension 0
There are 2 independent parts, one for each index of `group`. A program takes and returns all parts, laid end to end along the dimension named above; an argument that names none is the same for every part. Nothing has to cross between parts.
Inputs may be any that keep to these rules, and one draw needn't show every extreme that they name: `clip_index`: clip numbers never fall along the frames; each clip holds 1 to 3 consecutive frames.
All inputs are finite; a program needn't handle non-finite values.
Results may differ from a plain program's by a relative error of at most 0.01.
Values may be sent and summed in bfloat16 or wider, within the bound.
No kernel may reach another device: no remote copies, remote signals or barrier semaphores. Data moves between devices by JAX's collectives and lax.ppermute only.
A program may use at most 128 MiB of HBM per device.

v0:
```python
import jax
import jax.numpy as jnp
from jax import lax
from jax.sharding import PartitionSpec as P

CLAT = 16
CH = 384
PATCH = 16
STRIPS = 8
TF = 2
WS = 16
HL = 48


def shifted(value, axis, by):
    length = lax.axis_size(axis)
    return lax.ppermute(value, axis, [(i, (i + by) % length) for i in range(length)])


def partner(value, axis, apart):
    return lax.ppermute(value, axis, [(i, i ^ 1 << apart) for i in range(lax.axis_size(axis))])


def norm_act(values, gain):
    scale = lax.rsqrt(jnp.mean(values * values, axis=-1, keepdims=True) + 1e-06)
    return jax.nn.silu(values * scale * gain)


def extend(field, column, older):
    left = shifted(field[:, :, -1:], "tile", 1)
    left = jnp.where(column > 0, left, jnp.zeros_like(left))
    right = shifted(field[:, :, :1], "tile", -1)
    right = jnp.where(column < STRIPS - 1, right, jnp.zeros_like(right))
    wide = jnp.concatenate([left, field, right], axis=2)
    cache = shifted(field, "tile", STRIPS)
    corner_left = shifted(field[-2:, :, -1:], "tile", STRIPS + 1)
    corner_left = jnp.where(column > 0, corner_left, jnp.zeros_like(corner_left))
    corner_right = shifted(field[-2:, :, :1], "tile", STRIPS - 1)
    corner_right = jnp.where(column < STRIPS - 1, corner_right, jnp.zeros_like(corner_right))
    older = jnp.concatenate([corner_left, cache, corner_right], axis=2)
    return jnp.concatenate([older, wide], axis=0)


def causal_conv(full, keep, weight):
    frames = full.shape[0] - 2
    height = full.shape[1]
    width = full.shape[2] - 2
    channels = full.shape[3]
    outs = weight.shape[-1]
    padded = jnp.pad(full, ((0, 0), (1, 1), (0, 0), (0, 0)))
    total = jnp.zeros((frames * height * width, outs), jnp.float32)
    for step_t in range(3):
        slab = (
            padded[step_t : step_t + frames]
            * keep[:, step_t].astype(full.dtype)[:, None, None, None]
        )
        for step_r in range(3):
            rows = slab[:, step_r : step_r + height]
            stacked = jnp.concatenate(
                [rows[:, :, step_c : step_c + width] for step_c in range(3)], axis=-1
            )
            stacked = stacked.reshape(-1, 3 * channels)
            total = total + jnp.dot(
                stacked,
                weight[step_t, step_r].reshape(3 * channels, outs),
                preferred_element_type=jnp.float32,
            )
    return total.reshape(frames, height, width, outs)


def per_device(latents, clip_index, first_conv, first_gain, middle_conv, head_gain, head_weight):
    place = lax.axis_index("tile")
    tile_count = lax.axis_size("tile")
    offset = STRIPS // 2 - 1
    rotated = (place - offset) % tile_count
    column = rotated % STRIPS
    block = rotated // STRIPS
    seq_column = place % STRIPS
    shard_rows = latents.shape[0]
    pieces = latents.reshape(shard_rows, CLAT, STRIPS, WS).transpose(2, 0, 1, 3)
    order = jnp.bitwise_xor(seq_column, jnp.arange(STRIPS, dtype=jnp.int32))
    buffer = jnp.take(pieces, order, axis=0)
    for bit in range(STRIPS.bit_length() - 1):
        view = buffer.reshape((STRIPS >> bit + 1, 2, 1 << bit) + buffer.shape[1:])
        came = partner(view[:, 1], "tile", bit)
        buffer = jnp.stack([view[:, 0], came], axis=1).reshape(buffer.shape)
    gathered = jnp.take(buffer, order, axis=0)
    gathered = shifted(gathered, "tile", offset)
    video = gathered.reshape(TF, HL, CLAT, WS).transpose(0, 1, 3, 2)
    padded_ids = jnp.concatenate([jnp.full((4,), -1, jnp.int32), clip_index])
    window = lax.dynamic_slice_in_dim(padded_ids, block * TF + 2, TF + 2)
    keep = jnp.stack([window[step_t : step_t + TF] == window[2:] for step_t in range(3)], axis=1)
    first = causal_conv(extend(video, column, None), keep, first_conv).astype(jnp.bfloat16)
    active = norm_act(first.astype(jnp.float32), first_gain).astype(jnp.bfloat16)
    summed = first.astype(jnp.float32) + causal_conv(
        extend(active, column, None), keep, middle_conv
    )
    outward = norm_act(summed, head_gain).astype(jnp.bfloat16)
    patch = jnp.dot(outward.reshape(-1, CH), head_weight, preferred_element_type=jnp.float32)
    patch = patch.reshape(TF, HL, WS, 3, PATCH)
    half = PATCH // 2
    front = patch[..., :half]
    back = patch[..., half:]
    arrived = shifted(back[:, :, -1], "tile", 1)
    arrived = jnp.where(column > 0, arrived, jnp.zeros_like(arrived))
    moved = jnp.concatenate([arrived[:, :, None], back[:, :, :-1]], axis=2)
    picture = (front + moved).transpose(0, 3, 1, 2, 4)
    return picture.reshape(1, TF, 3, HL, WS * half)


def solution(mesh):
    placed = (P(("group", "tile"), None, None), P("group"), P(), P(), P(), P(), P())
    return jax.shard_map(
        per_device,
        mesh=mesh,
        in_specs=placed,
        out_specs=P(("group", "tile"), None, None, None, None),
        check_vma=False,
    )
```

profile of v0, /device:TPU:0, one launch (start us, length us, event | category | flops | bytes accessed | tf_op | source)
XLA Modules:
  0.0 194.8 jit_solution(11909733101809147580)
XLA Ops:
  3.7 2.9 %collective-permute-start.1 = (bf16[2,2,12,16,16]{4,3,2,0,1:T(8,128)(2,1)S(1)}, bf16[2,2,12,16,16]{4,3,2,0,1:T(8,128)(2,1)S(1)}, u32[]{:S(2)}, u32[]{:S(2)}) collective-permute-start(bf16[2,2,12,16,16]{4,3,2,0,1:T(8,128)(2,1)S(1)} %get-tuple-element.46), channel_id=1, source_target_pairs={{0,2},{1,3},{2,0},{3,1},{4,6},{5,7},{6,4},{7,5},{8,10},{9,11},{10,... | collective-permute-start | bytes 73736 | tf_op jit(solution)/shard_map/ppermute | solution.py:21
  6.6 5.2 %collective-permute-done.1 = bf16[2,2,12,16,16]{4,3,2,0,1:T(8,128)(2,1)S(1)} collective-permute-done((bf16[2,2,12,16,16]{4,3,2,0,1:T(8,128)(2,1)S(1)}, bf16[2,2,12,16,16]{4,3,2,0,1:T(8,128)(2,1)S(1)}, u32[]{:S(2)}, u32[]{:S(2)}) %collective-permute-start.1) | collective-permute-done | bytes 24608 | tf_op jit(solution)/shard_map/ppermute | solution.py:21
  14.6 3.9 %collective-permute-done.2 = bf16[1,4,12,16,16]{4,3,2,1,0:T(8,128)(2,1)S(1)} collective-permute-done((bf16[1,4,12,16,16]{4,3,2,1,0:T(8,128)(2,1)S(1)}, bf16[1,4,12,16,16]{4,3,2,1,0:T(8,128)(2,1)S(1)}, u32[]{:S(2)}, u32[]{:S(2)}) %collective-permute-start.2) | collective-permute-done | bytes 24608 | tf_op jit(solution)/shard_map/ppermute | solution.py:21
  19.4 8.9 %collective-permute-done.3 = bf16[8,12,16,16]{3,2,1,0:T(8,128)(2,1)S(1)} collective-permute-done((bf16[8,12,16,16]{3,2,1,0:T(8,128)(2,1)S(1)}, bf16[8,12,16,16]{3,2,1,0:T(8,128)(2,1)S(1)}, u32[]{:S(2)}, u32[]{:S(2)}) %collective-permute-start.3) | collective-permute-done | bytes 49184 | tf_op jit(solution)/shard_map/ppermute | solution.py:17
  28.7 4.1 %collective-permute-start.8 = (bf16[2,48,1,16]{1,0,2,3:T(2,128)(2,1)S(1)}, bf16[2,48,1,16]{1,0,2,3:T(2,128)(2,1)S(1)}, u32[]{:S(2)}, u32[]{:S(2)}) collective-permute-start(bf16[2,48,1,16]{1,0,2,3:T(2,128)(2,1)S(1)} %get-tuple-element.85), channel_id=1, source_target_pairs={{0,15},{1,0},{2,1},{3,2},{4,3},{5,4},{6,5},{7,6},{8,7},{9,8},{10,9... | collective-permute-start | bytes 9224 | tf_op jit(solution)/shard_map/ppermute | solution.py:17
  33.0 2.6 %collective-permute-start.5 = (bf16[2,48,16,16]{1,0,2,3:T(2,128)(2,1)S(1)}, bf16[2,48,16,16]{1,0,2,3:T(2,128)(2,1)S(1)}, u32[]{:S(2)}, u32[]{:S(2)}) collective-permute-start(bf16[2,48,16,16]{1,0,2,3:T(2,128)(2,1)S(1)} %bitcast.144), channel_id=1, source_target_pairs={{0,8},{1,9},{2,10},{3,11},{4,12},{5,13},{6,14},{7,15},{8,0},{9,1},... | collective-permute-start | bytes 147464 | tf_op jit(solution)/shard_map/ppermute | solution.py:17
  35.8 3.0 %collective-permute-start.4 = (bf16[2,48,1,16]{1,0,2,3:T(2,128)(2,1)S(1)}, bf16[2,48,1,16]{1,0,2,3:T(2,128)(2,1)S(1)}, u32[]{:S(2)}, u32[]{:S(2)}) collective-permute-start(bf16[2,48,1,16]{1,0,2,3:T(2,128)(2,1)S(1)} %get-tuple-element.84), channel_id=1, source_target_pairs={{0,9},{1,10},{2,11},{3,12},{4,13},{5,14},{6,15},{7,0},{8,1},{9,2},... | collective-permute-start | bytes 9224 | tf_op jit(solution)/shard_map/ppermute | solution.py:17
  38.8 2.7 %collective-permute-done.7 = bf16[2,48,1,16]{1,0,2,3:T(2,128)(2,1)S(1)} collective-permute-done((bf16[2,48,1,16]{1,0,2,3:T(2,128)(2,1)S(1)}, bf16[2,48,1,16]{1,0,2,3:T(2,128)(2,1)S(1)}, u32[]{:S(2)}, u32[]{:S(2)}) %collective-permute-start.7) | collective-permute-done | bytes 3104 | tf_op jit(solution)/shard_map/ppermute | solution.py:17
  61.7 2.6 %collective-permute-start.13 = (bf16[2,48,1,384]{3,2,1,0:T(2,128)(2,1)S(1)}, bf16[2,48,1,384]{3,2,1,0:T(2,128)(2,1)S(1)}, u32[]{:S(2)}, u32[]{:S(2)}) collective-permute-start(bf16[2,48,1,384]{3,2,1,0:T(2,128)(2,1)S(1)} %get-tuple-element.42), channel_id=1, source_target_pairs={{0,15},{1,0},{2,1},{3,2},{4,3},{5,4},{6,5},{7,6},{8,7},{9,8},{10,9... | collective-permute-start | bytes 221192 | tf_op jit(solution)/shard_map/ppermute | solution.py:17
  64.3 5.6 %fusion.21 = (bf16[1,1,3,384,384]{4,3,2,1,0:T(8,128)(2,1)S(1)}, bf16[1,1,3,384,384]{4,3,2,1,0:T(8,128)(2,1)}, bf16[1,1,3,384,384]{4,3,2,1,0:T(8,128)(2,1)}, bf16...) fusion(bf16[3,3,3,384,384]{4,3,2,1,0:T(8,128)(2,1)} %param.13), kind=kLoop, calls=%fused_computation.104 | loop fusion | bytes 15925248 | tf_op jit(solution)/shard_map/slice | solution.py:65
  70.5 2.2 %collective-permute-start.12 = (bf16[2,48,1,384]{3,2,1,0:T(2,128)(2,1)S(1)}, bf16[2,48,1,384]{3,2,1,0:T(2,128)(2,1)S(1)}, u32[]{:S(2)}, u32[]{:S(2)}) collective-permute-start(bf16[2,48,1,384]{3,2,1,0:T(2,128)(2,1)S(1)} %get-tuple-element.41), channel_id=1, source_target_pairs={{0,1},{1,2},{2,3},{3,4},{4,5},{5,6},{6,7},{7,8},{8,9},{9,10},{10,1... | collective-permute-start | bytes 221192 | tf_op jit(solution)/shard_map/ppermute | solution.py:17
  73.4 34.5 %collective-permute-done.11 = bf16[2,48,1,384]{3,2,1,0:T(2,128)(2,1)S(1)} collective-permute-done((bf16[2,48,1,384]{3,2,1,0:T(2,128)(2,1)S(1)}, bf16[2,48,1,384]{3,2,1,0:T(2,128)(2,1)S(1)}, u32[]{:S(2)}, u32[]{:S(2)}) %collective-permute-start.11) | collective-permute-done | bytes 73760 | tf_op jit(solution)/shard_map/ppermute | solution.py:17
  110.2 21.1 %collective-permute-done.10 = bf16[2,48,16,384]{3,2,1,0:T(8,128)(2,1)S(1)} collective-permute-done((bf16[2,48,16,384]{3,2,1,0:T(8,128)(2,1)S(1)}, bf16[2,48,16,384]{3,2,1,0:T(8,128)(2,1)S(1)}, u32[]{:S(2)}, u32[]{:S(2)}) %collective-permute-start.10) | collective-permute-done | bytes 1179680 | tf_op jit(solution)/shard_map/ppermute | solution.py:17
  131.4 2.3 %fusion.1 = bf16[4,50,18,384]{3,2,1,0:T(8,128)(2,1)S(1)} fusion(bf16[2,48,1,384]{3,2,1,0:T(2,128)(2,1)S(1)} %broadcast_select_fusion.2, bf16[2,48,1,384]{3,2,1,0:T(2,128)(2,1)S(1)} %broadcast_select_fusion.3, bf16[2,48,16,384]{3,2,1,0:T(8,128)(2,1)S(1)} %multiply_convert_fusion.1, bf16[2,48,1,384]{3,2,1,0:T(2,128)(2,1)S(1)} %broadcast_select_fusion.4, ...), kind=kLoop, calls=%fused_computation.6 | loop fusion | flops 29030400 | bytes 5419008 | tf_op jit(solution)/shard_map/concatenate | solution.py:41
  135.8 4.3 %fusion.24 = (bf16[2,48,16,384]{3,2,1,0:T(8,128)(2,1)S(1)}, bf16[2,48,16,384]{3,2,1,0:T(8,128)(2,1)S(1)}, bf16[2,48,16,384]{3,2,1,0:T(8,128)(2,1)S(1)}, bf16[2,4...) fusion(bf16[2,50,18,384]{3,2,1,0:T(8,128)(2,1)S(1)} %get-tuple-, ...), kind=kLoop, calls=%fused_computation.107 | loop fusion | bytes 21233664 | tf_op jit(solution)/shard_map/slice | solution.py:60
  140.1 2.4 %fusion.23 = (bf16[2,48,16,384]{3,2,1,0:T(8,128)(2,1)S(1)}, bf16[2,48,16,384]{3,2,1,0:T(8,128)(2,1)S(1)}, bf16[2,48,16,384]{3,2,1,0:T(8,128)(2,1)S(1)}, bf16[2,4...) fusion(bf16[2,50,18,384]{3,2,1,0:T(8,128)(2,1)S(1)} %get-tuple-, ...), kind=kLoop, calls=%fused_computation.106 | loop fusion | bytes 21233664 | tf_op jit(solution)/shard_map/slice | solution.py:60
  153.6 2.1 %convolution_add_fusion.13 = f32[1536,384]{1,0:T(8,128)S(1)} fusion(f32[1536,384]{1,0:T(8,128)S(1)} %convolution_add_fusion.14, bf16[1536,1152]{1,0:T(8,128)(2,1)S(1)} %bitcast.120, bf16[1152,384]{1,0:T(8,128)(2,1)S(1)} %bitcast.150), kind=kOutput, calls=%fused_computation.39 | convolution fusion | flops 1359544320 | bytes 9142272 | tf_op jit(solution)/shard_map/dot_general | solution.py:63
  156.9 2.2 %convolution_add_fusion.12 = f32[1536,384]{1,0:T(8,128)S(1)} fusion(f32[1536,384]{1,0:T(8,128)S(1)} %convolution_add_fusion.13, bf16[1536,1152]{1,0:T(8,128)(2,1)S(1)} %bitcast.121, bf16[1152,384]{1,0:T(8,128)(2,1)S(1)} %bitcast.149), kind=kOutput, calls=%fused_computation.38 | convolution fusion | flops 1359544320 | bytes 9142272 | tf_op jit(solution)/shard_map/dot_general | solution.py:63
  160.2 2.1 %convolution_add_fusion.11 = f32[1536,384]{1,0:T(8,128)S(1)} fusion(f32[1536,384]{1,0:T(8,128)S(1)} %convolution_add_fusion.12, bf16[1536,1152]{1,0:T(8,128)(2,1)S(1)} %bitcast.122, bf16[1152,384]{1,0:T(8,128)(2,1)S(1)} %bitcast.148), kind=kOutput, calls=%fused_computation.37 | convolution fusion | flops 1359544320 | bytes 9142272 | tf_op jit(solution)/shard_map/dot_general | solution.py:63
  168.9 2.6 %multiply_reduce_fusion = (f32[1536]{0:T(1024)S(1)}, f32[1536,384]{1,0:T(8,128)S(1)}) fusion(f32[1536,384]{1,0:T(8,128)S(1)} %get-tuple-element.89, f32[1536,384]{1,0:T(8,128)S(1)} %fusion.35, f32[1536,384]{1,0:T(8,128)S(1)} %convolution_add_fusion.9, bf16[1536,1152]{1,0:T(8,128)(2,1)S(1)} %bitcast.117, bf16[1152,384]{1,0:T(8,128)(2,1)S(1)} %bitcast.127), kind=kOutput, calls=%fused_computation.44 | convolution fusion | flops 1361902080 | bytes 13867008 | tf_op jit(solution)/shard_map/dot_general | solution.py:63
  172.3 2.2 %fusion.36 = f32[2,48,16,3,16]{2,4,3,1,0:T(8,128)S(1)} fusion(bf16[2,48,16,384,1]{3,2,4,1,0:T(8,128)(2,1)S(1)} %bitcast.118, bf16[3,16,384,1,1]{2,1,0,4,3:T(8,128)(2,1)S(1)} %bitcast.115), kind=kOutput, calls=%fused_computation.119 | convolution fusion | flops 56623104 | bytes 1511424 | tf_op jit(solution)/shard_map/dot_general | solution.py:99
  177.8 5.0 %collective-permute-start.14 = (f32[2,48,3,8]{1,3,2,0:T(8,128)S(1)}, f32[2,48,3,8]{1,3,2,0:T(8,128)S(1)}, u32[]{:S(2)}, u32[]{:S(2)}) collective-permute-start(f32[2,48,3,8]{1,3,2,0:T(8,128)S(1)} %bitcast.168), channel_id=1, source_target_pairs={{0,1},{1,2},{2,3},{3,4},{4,5},{5,6},{6,7},{7,8},{8,9},{9,10},{10,1... | collective-permute-start | bytes 27656 | tf_op jit(solution)/shard_map/ppermute | solution.py:17
  183.9 3.6 %collective-permute-done.14 = f32[2,48,3,8]{1,3,2,0:T(8,128)S(1)} collective-permute-done((f32[2,48,3,8]{1,3,2,0:T(8,128)S(1)}, f32[2,48,3,8]{1,3,2,0:T(8,128)S(1)}, u32[]{:S(2)}, u32[]{:S(2)}) %collective-permute-start.14) | collective-permute-done | bytes 9248 | tf_op jit(solution)/shard_map/ppermute | solution.py:17
  189.0 3.1 %fusion.11 = f32[2,3,48,16,8]{3,4,1,2,0:T(8,128)} fusion(f32[2,48,16,3,16]{2,4,3,1,0:T(8,128)S(1)} %fusion.36, f32[2,48,15,3,8]{2,4,3,1,0:T(8,128)} %slice.548, f32[2,48,1,3,8]{2,4,3,1,0:T(8,128)} %copy.139), kind=kLoop, calls=%fused_computation.50 | loop fusion | flops 73728 | bytes 442368 | tf_op jit(solution)/shard_map/transpose | solution.py:107
  (167 shorter events, 62.4 us)
Async XLA Ops:
  0.0 172.3 %copy-start = (bf16[384,48]{0,1:T(8,128)(2,1)S(1)}, bf16[384,48]{0,1:T(8,128)(2,1)}, u32[]{:S(2)}) copy-start(bf16[384,48]{0,1:T(8,128)(2,1)} %param.15) | copy-start | bytes 110596
  1.8 12.1 %copy-start.15 = (bf16[3,3,3,16,384]{4,3,2,1,0:T(8,128)(2,1)S(1)}, bf16[3,3,3,16,384]{4,3,2,1,0:T(8,128)(2,1)}, u32[]{:S(2)}) copy-start(bf16[3,3,3,16,384]{4,3,2,1,0:T(8,128)(2,1)} %param.11) | copy-start | bytes 995332
  2.0 1.6 collective-permute-start
  3.7 8.1 %collective-permute-start.1 = (bf16[2,2,12,16,16]{4,3,2,0,1:T(8,128)(2,1)S(1)}, bf16[2,2,12,16,16]{4,3,2,0,1:T(8,128)(2,1)S(1)}, u32[]{:S(2)}, u32[]{:S(2)}) collective-permute-start(bf16[2,2,12,16,16]{4,3,2,0,1:T(8,128)(2,1)S(1)} %get-tuple-element.46), channel_id=1, source_target_pairs={{0,2},{1,3},{2,0},{3,1},{4,6},{5,7},{6,4},{7,5},{8,10},{9,11},{10,... | collective-permute-start | bytes 73736 | tf_op jit(solution)/shard_map/ppermute | solution.py:21
  11.9 7.4 %copy-start.28 = (s32[4]{0:T(128)S(1)}, s32[4]{0:T(128)}, u32[]{:S(2)}) copy-start(s32[4]{0:T(128)} %param.10) | copy-start | bytes 52
  12.0 6.4 %collective-permute-start.2 = (bf16[1,4,12,16,16]{4,3,2,1,0:T(8,128)(2,1)S(1)}, bf16[1,4,12,16,16]{4,3,2,1,0:T(8,128)(2,1)S(1)}, u32[]{:S(2)}, u32[]{:S(2)}) collective-permute-start(bf16[1,4,12,16,16]{4,3,2,1,0:T(8,128)(2,1)S(1)} %get-tuple-element.44), channel_id=1, source_target_pairs={{0,4},{1,5},{2,6},{3,7},{4,0},{5,1},{6,2},{7,3},{8,12},{9,13},{10,... | collective-permute-start | bytes 73736 | tf_op jit(solution)/shard_map/ppermute | solution.py:21
  19.3 9.1 %collective-permute-start.3 = (bf16[8,12,16,16]{3,2,1,0:T(8,128)(2,1)S(1)}, bf16[8,12,16,16]{3,2,1,0:T(8,128)(2,1)S(1)}, u32[]{:S(2)}, u32[]{:S(2)}) collective-permute-start(bf16[8,12,16,16]{3,2,1,0:T(8,128)(2,1)S(1)} %broadcast_select_fusion.1), channel_id=1, source_target_pairs={{0,3},{1,4},{2,5},{3,6},{4,7},{5,8},{6,9},{7,10},{8,11},{9,12},{10... | collective-permute-start | bytes 147464 | tf_op jit(solution)/shard_map/ppermute | solution.py:17
  28.7 10.0 %collective-permute-start.8 = (bf16[2,48,1,16]{1,0,2,3:T(2,128)(2,1)S(1)}, bf16[2,48,1,16]{1,0,2,3:T(2,128)(2,1)S(1)}, u32[]{:S(2)}, u32[]{:S(2)}) collective-permute-start(bf16[2,48,1,16]{1,0,2,3:T(2,128)(2,1)S(1)} %get-tuple-element.85), channel_id=1, source_target_pairs={{0,15},{1,0},{2,1},{3,2},{4,3},{5,4},{6,5},{7,6},{8,7},{9,8},{10,9... | collective-permute-start | bytes 9224 | tf_op jit(solution)/shard_map/ppermute | solution.py:17
  32.9 11.7 %copy-start.22 = (bf16[2]{0:T(256)(128)(2,1)}, bf16[2]{0:T(256)(128)(2,1)S(1)}, u32[]{:S(2)}) copy-start(bf16[2]{0:T(256)(128)(2,1)S(1)} %get-tuple-element.86) | copy-start | bytes 16
  32.9 11.7 %copy-start.24 = (bf16[2]{0:T(256)(128)(2,1)}, bf16[2]{0:T(256)(128)(2,1)S(1)}, u32[]{:S(2)}) copy-start(bf16[2]{0:T(256)(128)(2,1)S(1)} %get-tuple-element.87) | copy-start | bytes 16
  32.9 5.9 %collective-permute-start.6 = (bf16[2,48,1,16]{1,0,2,3:T(2,128)(2,1)S(1)}, bf16[2,48,1,16]{1,0,2,3:T(2,128)(2,1)S(1)}, u32[]{:S(2)}, u32[]{:S(2)}) collective-permute-start(bf16[2,48,1,16]{1,0,2,3:T(2,128)(2,1)S(1)} %get-tuple-element.85), channel_id=1, source_target_pairs={{0,7},{1,8},{2,9},{3,10},{4,11},{5,12},{6,13},{7,14},{8,15},{9,0},... | collective-permute-start | bytes 9224 | tf_op jit(solution)/shard_map/ppermute | solution.py:17
  33.0 10.4 %collective-permute-start.5 = (bf16[2,48,16,16]{1,0,2,3:T(2,128)(2,1)S(1)}, bf16[2,48,16,16]{1,0,2,3:T(2,128)(2,1)S(1)}, u32[]{:S(2)}, u32[]{:S(2)}) collective-permute-start(bf16[2,48,16,16]{1,0,2,3:T(2,128)(2,1)S(1)} %bitcast.144), channel_id=1, source_target_pairs={{0,8},{1,9},{2,10},{3,11},{4,12},{5,13},{6,14},{7,15},{8,0},{9,1},... | collective-permute-start | bytes 147464 | tf_op jit(solution)/shard_map/ppermute | solution.py:17
  35.6 5.9 %collective-permute-start.7 = (bf16[2,48,1,16]{1,0,2,3:T(2,128)(2,1)S(1)}, bf16[2,48,1,16]{1,0,2,3:T(2,128)(2,1)S(1)}, u32[]{:S(2)}, u32[]{:S(2)}) collective-permute-start(bf16[2,48,1,16]{1,0,2,3:T(2,128)(2,1)S(1)} %get-tuple-element.84), channel_id=1, source_target_pairs={{0,1},{1,2},{2,3},{3,4},{4,5},{5,6},{6,7},{7,8},{8,9},{9,10},{10,1... | collective-permute-start | bytes 9224 | tf_op jit(solution)/shard_map/ppermute | solution.py:17
  35.8 5.8 %collective-permute-start.4 = (bf16[2,48,1,16]{1,0,2,3:T(2,128)(2,1)S(1)}, bf16[2,48,1,16]{1,0,2,3:T(2,128)(2,1)S(1)}, u32[]{:S(2)}, u32[]{:S(2)}) collective-permute-start(bf16[2,48,1,16]{1,0,2,3:T(2,128)(2,1)S(1)} %get-tuple-element.84), channel_id=1, source_target_pairs={{0,9},{1,10},{2,11},{3,12},{4,13},{5,14},{6,15},{7,0},{8,1},{9,2},... | collective-permute-start | bytes 9224 | tf_op jit(solution)/shard_map/ppermute | solution.py:17
  52.1 3.1 %copy-start.21 = (bf16[1,1,3,16,384]{4,3,2,1,0:T(8,128)(2,1)S(1)}, bf16[1,1,3,16,384]{4,3,2,1,0:T(8,128)(2,1)}, u32[]{:S(2)}) copy-start(bf16[1,1,3,16,384]{4,3,2,1,0:T(8,128)(2,1)} %get-tuple-element.55) | copy-start | bytes 110596
  61.7 11.6 %collective-permute-start.13 = (bf16[2,48,1,384]{3,2,1,0:T(2,128)(2,1)S(1)}, bf16[2,48,1,384]{3,2,1,0:T(2,128)(2,1)S(1)}, u32[]{:S(2)}, u32[]{:S(2)}) collective-permute-start(bf16[2,48,1,384]{3,2,1,0:T(2,128)(2,1)S(1)} %get-tuple-element.42), channel_id=1, source_target_pairs={{0,15},{1,0},{2,1},{3,2},{4,3},{5,4},{6,5},{7,6},{8,7},{9,8},{10,9... | collective-permute-start | bytes 221192 | tf_op jit(solution)/shard_map/ppermute | solution.py:17
  69.9 38.0 %collective-permute-start.11 = (bf16[2,48,1,384]{3,2,1,0:T(2,128)(2,1)S(1)}, bf16[2,48,1,384]{3,2,1,0:T(2,128)(2,1)S(1)}, u32[]{:S(2)}, u32[]{:S(2)}) collective-permute-start(bf16[2,48,1,384]{3,2,1,0:T(2,128)(2,1)S(1)} %get-tuple-element.42), channel_id=1, source_target_pairs={{0,7},{1,8},{2,9},{3,10},{4,11},{5,12},{6,13},{7,14},{8,15},{9,0},... | collective-permute-start | bytes 221192 | tf_op jit(solution)/shard_map/ppermute | solution.py:17
  70.0 61.4 %collective-permute-start.10 = (bf16[2,48,16,384]{3,2,1,0:T(8,128)(2,1)S(1)}, bf16[2,48,16,384]{3,2,1,0:T(8,128)(2,1)S(1)}, u32[]{:S(2)}, u32[]{:S(2)}) collective-permute-start(bf16[2,48,16,384]{3,2,1,0:T(8,128)(2,1)S(1)} %multiply_convert_fusion.1), channel_id=1, source_target_pairs={{0,8},{1,9},{2,10},{3,11},{4,12},{5,13},{6,14},{7,15},{8,0},{9,1},... | collective-permute-start | bytes 3538952 | tf_op jit(solution)/shard_map/ppermute | solution.py:17
  70.5 37.6 %collective-permute-start.12 = (bf16[2,48,1,384]{3,2,1,0:T(2,128)(2,1)S(1)}, bf16[2,48,1,384]{3,2,1,0:T(2,128)(2,1)S(1)}, u32[]{:S(2)}, u32[]{:S(2)}) collective-permute-start(bf16[2,48,1,384]{3,2,1,0:T(2,128)(2,1)S(1)} %get-tuple-element.41), channel_id=1, source_target_pairs={{0,1},{1,2},{2,3},{3,4},{4,5},{5,6},{6,7},{7,8},{8,9},{9,10},{10,1... | collective-permute-start | bytes 221192 | tf_op jit(solution)/shard_map/ppermute | solution.py:17
  72.7 35.6 %collective-permute-start.9 = (bf16[2,48,1,384]{3,2,1,0:T(2,128)(2,1)S(1)}, bf16[2,48,1,384]{3,2,1,0:T(2,128)(2,1)S(1)}, u32[]{:S(2)}, u32[]{:S(2)}) collective-permute-start(bf16[2,48,1,384]{3,2,1,0:T(2,128)(2,1)S(1)} %get-tuple-element.41), channel_id=1, source_target_pairs={{0,9},{1,10},{2,11},{3,12},{4,13},{5,14},{6,15},{7,0},{8,1},{9,2},... | collective-permute-start | bytes 221192 | tf_op jit(solution)/shard_map/ppermute | solution.py:17
  143.7 2.1 %copy-start.6 = (bf16[2,48,16,384]{3,2,1,0:T(8,128)(2,1)S(1)}, bf16[2,48,16,384]{3,2,1,0:T(8,128)(2,1)}, u32[]{:S(2)}) copy-start(bf16[2,48,16,384]{3,2,1,0:T(8,128)(2,1)} %get-tuple-element.40) | copy-start | bytes 3538948
  147.0 2.1 %copy-start.3 = (bf16[2,48,16,384]{3,2,1,0:T(8,128)(2,1)S(1)}, bf16[2,48,16,384]{3,2,1,0:T(8,128)(2,1)}, u32[]{:S(2)}) copy-start(bf16[2,48,16,384]{3,2,1,0:T(8,128)(2,1)} %get-tuple-element.37) | copy-start | bytes 3538948
  168.9 2.7 %copy-start.27 = (f32[384]{0:T(512)S(1)}, f32[384]{0:T(512)}, u32[]{:S(2)}) copy-start(f32[384]{0:T(512)} %param.14) | copy-start | bytes 4612
  177.8 9.7 %collective-permute-start.14 = (f32[2,48,3,8]{1,3,2,0:T(8,128)S(1)}, f32[2,48,3,8]{1,3,2,0:T(8,128)S(1)}, u32[]{:S(2)}, u32[]{:S(2)}) collective-permute-start(f32[2,48,3,8]{1,3,2,0:T(8,128)S(1)} %bitcast.168), channel_id=1, source_target_pairs={{0,1},{1,2},{2,3},{3,4},{4,5},{5,6},{6,7},{7,8},{8,9},{9,10},{10,1... | collective-permute-start | bytes 27656 | tf_op jit(solution)/shard_map/ppermute | solution.py:17
  (20 other events, 25.7 us)
where the time goes:
time: 198 us; the launch traced here: 195 us
  waiting for transfers between devices  81.5 us (41%)
  local copies, waits for them, and re-layouts  41.1 us (21%)
  matrix products  26.8 us (14%)
  starting transfers between devices  26.2 us (13%)
  other arithmetic  18.1 us (9%)
    ppermute x12, waiting for transfers between devices, shifted(): lax.ppermute(value, axis, [(i, (i + by) % length) for i in range(length)])  71.4 us
    dot_general x18, matrix products, causal_conv(): jnp.dot(stacked, weight[step_t, step_r].reshape(3 * channels, outs), pref...  24.6 us
    ppermute x12, starting transfers between devices, shifted(): lax.ppermute(value, axis, [(i, (i + by) % length) for i in range(length)])  20.8 us
    slice x5, local copies, waits for them, and re-layouts, causal_conv(): rows[:, :, step_c:step_c + width]  10.6 us
    ppermute x3, waiting for transfers between devices, partner(): lax.ppermute(value, axis, [(i, i ^ 1 << apart) for i in range(lax.axis_si...  10.1 us
    concatenate x17, other arithmetic, causal_conv(): jnp.concatenate([rows[:, :, step_c:step_c + width] for step_c in range(3)...  9.24 us
    unnamed x58, local copies, waits for them, and re-layouts  7.46 us
    slice x2, local copies, waits for them, and re-layouts, causal_conv(): weight[step_t, step_r].reshape(3 * channels, outs)  6.3 us
  transfers between devices with their start and end apart: 15, of which 9 were waited for; matrix products, arithmetic and copies ran while one was open for 6% of the time, Pallas kernels for 0%

commit v1 on v0

v1 whole, which is shorter than its diff:
```python
import functools

import jax
import jax.numpy as jnp
from jax import lax
from jax.experimental import pallas as pl
from jax.experimental.pallas import tpu as pltpu
from jax.sharding import PartitionSpec as P

CLAT = 16
CH = 384
PATCH = 16
STRIPS = 8
TF = 2
WS = 16
HL = 48
LANE = 128
PER_TILE = LANE // CLAT
TILES_WIN = 4
PAIRS = 10
COLS = 2 * PAIRS
OUT_COLS = WS + 1
CELLS = PAIRS * HL
OUT_CELLS = OUT_COLS * HL
PAD = 8
LT = CH // LANE


def silu(v):
    half = 0.5 * v
    return half + half * jnp.tanh(half)


def inv_rms(x):
    return lax.rsqrt(jnp.mean(x * x, axis=-1, keepdims=True) + 1e-06)


def decode_kernel(
    slots,
    place_ref,
    clip_ref,
    recv_ref,
    fc_ref,
    fg_ref,
    mc_ref,
    hg_ref,
    hw_ref,
    out_ref,
    wbuf,
    b1,
    vf,
    x1,
    act,
    first,
    xw,
    ysum,
    wsem,
):
    f32, bf16 = jnp.float32, jnp.bfloat16
    copies = []
    for dt, dest in ((0, 0), (1, 1), (2, 3)):
        for dr in range(3):
            for dc in range(3):
                copy = pltpu.make_async_copy(
                    mc_ref.at[dt, dr, dc],
                    wbuf.at[dest, pl.ds((dc * 3 + dr) * CH, CH)],
                    wsem.at[dt * 9 + dr * 3 + dc],
                )
                copy.start()
                copies.append(copy)

    place = place_ref[0]
    tiles = recv_ref.shape[0]
    rotated = lax.rem(place - (STRIPS // 2 - 1) + tiles, tiles)
    column = lax.rem(rotated, STRIPS)
    block = lax.div(rotated, STRIPS)
    ids = []
    for slot in range(6):
        frame = block * TF - 4 + slot
        known = clip_ref[jnp.maximum(frame, 0)]
        ids.append(jnp.where(frame >= 0, known, -1))
    inner_left = jnp.where(column > 0, 1.0, 0.0).astype(f32)
    inner_right = jnp.where(column < STRIPS - 1, 1.0, 0.0).astype(f32)

    b1[...] = jnp.zeros_like(b1)
    for dt in range(3):
        for dr in range(3):
            taps = fc_ref[dt * 3 + dr]
            b1[dt, dr * 64 : dr * 64 + 48, :CH] = taps
            b1[dt, dr * 64 + 16 : dr * 64 + 64, CH:] = taps

    vf[...] = jnp.zeros_like(vf)
    for slot in range(6 - slots, 6):
        base = jnp.maximum(block * TF - 4 + slot, 0) * 4
        for quarter in range(4):
            for tile in range(TILES_WIN):
                vf[PAD + 12 * quarter : PAD + 12 * quarter + 12, tile * LANE : (tile + 1) * LANE] = (
                    recv_ref[base + quarter, tile].astype(f32)
                )
        rows = [vf[PAD - 1 + dr : PAD - 1 + dr + HL, :] for dr in range(3)]
        for pair in range(PAIRS):
            at = 32 * pair + 80
            x1[slot - 6 + slots, pair * HL : (pair + 1) * HL, :] = jnp.concatenate(
                [row[:, at : at + 64] for row in rows], axis=-1
            ).astype(bf16)

    act[...] = jnp.zeros_like(act)
    gain = fg_ref[...]
    for t in range(4):
        total = None
        for dt in range(3):
            slot = t + dt
            if slot < 6 - slots:
                continue
            left = x1[slot - 6 + slots]
            if dt < 2:
                left = left * jnp.where(ids[slot] == ids[t + 2], 1.0, 0.0).astype(bf16)
            part = jnp.dot(left, b1[dt], preferred_element_type=f32)
            total = part if total is None else total + part
        for side in range(2):
            rounded = total[:, side * CH : (side + 1) * CH].astype(bf16)
            if t >= 2:
                for pair in range(PAIRS):
                    first[t - 2, (2 * pair + side) * HL : (2 * pair + side + 1) * HL, :] = rounded[
                        pair * HL : (pair + 1) * HL
                    ]
            x = rounded.astype(f32)
            a = silu(x * inv_rms(x) * gain)
            for pair in range(PAIRS):
                piece = a[pair * HL : (pair + 1) * HL]
                if pair == 0:
                    piece = piece * inner_left
                if pair == PAIRS - 1:
                    piece = piece * inner_right
                for lt in range(LT):
                    act[t, 2 * pair + side, lt, PAD : PAD + HL, :] = piece[:, lt * LANE : (lt + 1) * LANE]

    same = jnp.where(ids[4] == ids[5], 1.0, 0.0).astype(f32)
    keep0 = jnp.where(ids[2] == ids[4], 1.0, 0.0).astype(f32)
    keep1 = jnp.where(ids[3] == ids[4], 1.0, 0.0).astype(f32)
    whole = 1.0 - 0.5 * same
    half = 0.5 * same

    def transform(j, carry):
        at = pl.multiple_of(j * HL, HL)
        for dr in range(3):
            for lt in range(LT):
                d = [act[t, j, lt, PAD - 1 + dr : PAD - 1 + dr + HL, :].astype(bf16).astype(f32) for t in range(4)]
                d1 = d[1] * keep1
                mixed = (
                    d[0] * keep0 - same * d[2],
                    whole * d1 + half * d[2],
                    whole * d[2] - half * d1,
                    d[3] - same * d1,
                )
                lanes = slice((dr * LT + lt) * LANE, (dr * LT + lt + 1) * LANE)
                for m in range(4):
                    xw[m, pl.ds(at, HL), lanes] = mixed[m].astype(bf16)
        return carry

    lax.fori_loop(0, COLS, transform, 0)

    for copy in copies:
        copy.wait()

    def weights(i, carry):
        at = pl.multiple_of(i * LANE, LANE)
        g0 = wbuf[0, pl.ds(at, LANE), :].astype(f32)
        g1 = wbuf[1, pl.ds(at, LANE), :].astype(f32)
        g2 = wbuf[3, pl.ds(at, LANE), :].astype(f32)
        wbuf[1, pl.ds(at, LANE), :] = (g1 + same * (g0 + g2)).astype(bf16)
        wbuf[2, pl.ds(at, LANE), :] = (g2 + same * (g0 - g1)).astype(bf16)
        return carry

    lax.fori_loop(0, 9 * CH // LANE, weights, 0)

    ysum[...] = jnp.zeros_like(ysum)

    def products(m, carry):
        left = jnp.concatenate(
            [xw[m, (1 + dc - 1) * HL : (1 + dc - 1) * HL + OUT_CELLS, :] for dc in range(3)], axis=-1
        )
        part = jnp.dot(left, wbuf[m], preferred_element_type=f32)
        scale0 = jnp.where(m < 3, 1.0, 0.0).astype(f32)
        sign = jnp.where(m == 1, same, jnp.where(m == 2, -same, 0.0))
        scale1 = jnp.where(m == 3, 1.0, sign).astype(f32)
        ysum[0] += part * scale0
        ysum[1] += part * scale1
        return carry

    lax.fori_loop(0, 4, products, 0)

    hgain = hg_ref[...]
    lane = lax.broadcasted_iota(jnp.int32, (HL, LANE), 1)
    for t in range(2):
        x = ysum[t] + first[t, HL : HL + OUT_CELLS, :].astype(f32)
        outward = silu(x * inv_rms(x) * hgain).astype(bf16)
        patch = jnp.dot(outward, hw_ref[...], preferred_element_type=f32)
        for colour in range(3):
            sums = [jnp.zeros((HL, LANE), f32), jnp.zeros((HL, LANE), f32)]
            for w in range(-1, WS):
                cell = patch[(w + 1) * HL : (w + 2) * HL]
                if w < 0:
                    cell = cell * inner_left
                turned = pltpu.roll(cell, (8 * w - PATCH * colour) % LANE, 1)
                inside = (lane >= 8 * w) & (lane < 8 * w + PATCH)
                sums[w % 2] = jnp.where(inside, turned, sums[w % 2])
            out_ref[0, t, colour] = sums[0] + sums[1]


def per_device(latents, clip_index, first_conv, first_gain, middle_conv, head_gain, head_weight):
    tiles = lax.axis_size("tile")
    place = lax.axis_index("tile").astype(jnp.int32).reshape(1)
    rows = latents.shape[0]
    width = latents.shape[2]
    blocks = tiles // STRIPS
    slots = min(6, blocks * TF)
    packed = latents.reshape(rows, CLAT, width // PER_TILE, PER_TILE).transpose(2, 0, 3, 1)
    packed = packed.reshape(width // PER_TILE, rows, LANE)
    packed = jnp.pad(packed, ((1, 1), (0, 0), (0, 0)))
    sent = []
    for dest in range(tiles):
        strip = (dest - (STRIPS // 2 - 1)) % tiles % STRIPS
        sent.append(packed[2 * strip : 2 * strip + TILES_WIN])
    sent = jnp.stack(sent)
    came = lax.all_to_all(sent, "tile", 0, 0, tiled=True)

    vmem = pl.BlockSpec(memory_space=pltpu.VMEM)
    smem = pl.BlockSpec(memory_space=pltpu.SMEM)
    call = pl.pallas_call(
        functools.partial(decode_kernel, slots),
        out_shape=jax.ShapeDtypeStruct((1, TF, 3, HL, WS * PATCH // 2), jnp.float32),
        in_specs=[smem, smem, vmem, vmem, vmem, pl.BlockSpec(memory_space=pl.ANY), vmem, vmem],
        out_specs=vmem,
        scratch_shapes=[
            pltpu.VMEM((4, 9 * CH, CH), jnp.bfloat16),
            pltpu.VMEM((3, 192, 2 * CH), jnp.bfloat16),
            pltpu.VMEM((HL + 2 * PAD, TILES_WIN * LANE), jnp.float32),
            pltpu.VMEM((slots, CELLS, 192), jnp.bfloat16),
            pltpu.VMEM((4, COLS, LT, HL + 2 * PAD, LANE), jnp.float32),
            pltpu.VMEM((2, COLS * HL, CH), jnp.bfloat16),
            pltpu.VMEM((4, COLS * HL, 3 * CH), jnp.bfloat16),
            pltpu.VMEM((2, OUT_CELLS, CH), jnp.float32),
            pltpu.SemaphoreType.DMA((27,)),
        ],
        compiler_params=pltpu.CompilerParams(vmem_limit_bytes=60 * 1024 * 1024),
    )
    return call(
        place,
        clip_index,
        came,
        first_conv.reshape(9, 3 * CLAT, CH),
        first_gain.reshape(1, CH),
        middle_conv,
        head_gain.reshape(1, CH),
        jnp.pad(head_weight, ((0, 0), (0, LANE - 3 * PATCH))),
    )


def solution(mesh):
    placed = (P(("group", "tile"), None, None), P("group"), P(), P(), P(), P(), P())
    return jax.shard_map(
        per_device,
        mesh=mesh,
        in_specs=placed,
        out_specs=P(("group", "tile"), None, None, None, None),
        check_vma=False,
    )
```

time: 198 us -> 55.5 us (0.28); the launches traced: 195 us -> 55.2 us
  waiting for transfers between devices: 81.5 us -> 4.88 us
  matrix products: 26.8 us -> 0 us
  Pallas kernels: 0 us -> 26.2 us
  local copies, waits for them, and re-layouts: 41.1 us -> 16.6 us
  starting transfers between devices: 26.2 us -> 7.41 us
  other arithmetic: 18.1 us -> 0 us
    ppermute x15 -> x0, waiting for transfers between devices: 81.5 us -> none  [the longest x12 71.4 us: shifted(): lax.ppermute(value, axis, [(i, (i + by) % length) for i in range(length)])]
    dot_general x19 -> x0, matrix products: 26.8 us -> none  [the longest x18 24.6 us: causal_conv(): jnp.dot(stacked, weight[step_t, step_r].reshape(3 * channels, outs), pref...]
    pallas_call x0 -> x1, Pallas kernels: none -> 26.2 us  [per_device(): call(place, clip_index, came, first_conv.reshape(9, 3 * CLAT, CH), first_...]
    ppermute x15 -> x0, starting transfers between devices: 26.2 us -> none  [the longest x12 20.8 us: shifted(): lax.ppermute(value, axis, [(i, (i + by) % length) for i in range(length)])]
    slice x14 -> x1, local copies, waits for them, and re-layouts: 21.5 us -> 0.07 us  [per_device(): sent.append(packed[2 * strip:2 * strip + TILES_WIN])]
    concatenate x19 -> x0, other arithmetic: 11.7 us -> none  [the longest x17 9.24 us: causal_conv(): jnp.concatenate([rows[:, :, step_c:step_c + width] for step_c in range(3)...]
    all_to_all x0 -> x1, starting transfers between devices: none -> 7.41 us  [per_device(): came = lax.all_to_all(sent, 'tile', 0, 0, tiled=True)]
    concatenate x9 -> x0, local copies, waits for them, and re-layouts: 5.07 us -> none  [causal_conv(): jnp.concatenate([rows[:, :, step_c:step_c + width] for step_c in range(3)...]
  transfers between devices with their start and end apart: 15 -> 1, of which waited for: 9 -> 1; matrix products, arithmetic and copies ran while one was open for 6% -> 7% of each run, Pallas kernels for 0% -> 0%
where the time goes in v1:
time: 55.5 us; the launch traced here: 55.2 us
  Pallas kernels  26.2 us (47%)
  local copies, waits for them, and re-layouts  16.6 us (30%)
  starting transfers between devices  7.41 us (13%)
  waiting for transfers between devices  4.88 us (9%)
    pallas_call x1, Pallas kernels, per_device(): call(place, clip_index, came, first_conv.reshape(9, 3 * CLAT, CH), first_...  26.2 us
    unnamed x17, local copies, waits for them, and re-layouts  11 us
    all_to_all x1, starting transfers between devices, per_device(): came = lax.all_to_all(sent, 'tile', 0, 0, tiled=True)  7.41 us
    all_to_all x1, waiting for transfers between devices, per_device(): came = lax.all_to_all(sent, 'tile', 0, 0, tiled=True)  4.88 us
    another operation x7, local copies, waits for them, and re-layouts, per_device(): sent = jnp.stack(sent)  1.33 us
    reshape x1, local copies, waits for them, and re-layouts, per_device(): head_gain.reshape(1, CH)  1.27 us
    reshape x1, local copies, waits for them, and re-layouts, per_device(): first_gain.reshape(1, CH)  1.25 us
  transfers between devices with their start and end apart: 1, of which 1 were waited for; matrix products, arithmetic and copies ran while one was open for 7% of the time, Pallas kernels for 0%

profile of v1, /device:TPU:0, one launch (start us, length us, event | category | flops | bytes accessed | tf_op | source)
XLA Modules:
  0.0 55.2 jit_solution(5179005690061055768)
XLA Ops:
  0.0 1.0 %copy.25 = bf16[12,16,128]{1,2,0:T(8,128)(2,1)S(1)} copy(bf16[12,16,128]{2,1,0:T(8,128)(2,1)} %param.7) | data formatting | bytes 98304 | tf_op args[0]
  2.1 0.6 %constant_dynamic-update-slice_fusion.15 = bf16[16,4,12,128]{3,1,2,0:T(4,128)(2,1)} fusion(bf16[1,4,12,128]{3,1,2,0:T(4,128)(2,1)S(1)} %stack.35), kind=kLoop, calls=%fused_computation.17 | loop fusion | bytes 24576
  2.7 0.6 %constant_dynamic-update-slice_fusion.14 = bf16[16,4,12,128]{3,1,2,0:T(4,128)(2,1)} fusion(bf16[16,4,12,128]{3,1,2,0:T(4,128)(2,1)} %constant_dynamic-update-slice_fusion.15, bf16[1,4,12,128]{3,1,2,0:T(4,128)(2,1)S(1)} %stack.36), kind=kLoop, calls=%fused_computation.16 | loop fusion | bytes 24576
  3.3 0.6 %constant_dynamic-update-slice_fusion.13 = bf16[16,4,12,128]{3,1,2,0:T(4,128)(2,1)} fusion(bf16[16,4,12,128]{3,1,2,0:T(4,128)(2,1)} %constant_dynamic-update-slice_fusion.14, bf16[16,12,128]{2,0,1:T(8,128)(2,1)S(1)} %reshape.32), kind=kLoop, calls=%fused_computation.15 | loop fusion | bytes 61440
  3.9 0.6 %constant_dynamic-update-slice_fusion.12 = bf16[16,4,12,128]{3,1,2,0:T(4,128)(2,1)} fusion(bf16[16,4,12,128]{3,1,2,0:T(4,128)(2,1)} %constant_dynamic-update-slice_fusion.13, bf16[16,12,128]{2,0,1:T(8,128)(2,1)S(1)} %reshape.32), kind=kLoop, calls=%fused_computation.14 | loop fusion | bytes 61440
  4.5 0.6 %constant_dynamic-update-slice_fusion.11 = bf16[16,4,12,128]{3,1,2,0:T(4,128)(2,1)} fusion(bf16[16,4,12,128]{3,1,2,0:T(4,128)(2,1)} %constant_dynamic-update-slice_fusion.12, bf16[1,4,12,128]{3,1,2,0:T(4,128)(2,1)S(1)} %stack.39), kind=kLoop, calls=%fused_computation.13 | loop fusion | bytes 24576
  5.1 0.6 %constant_dynamic-update-slice_fusion.10 = bf16[16,4,12,128]{3,1,2,0:T(4,128)(2,1)} fusion(bf16[16,4,12,128]{3,1,2,0:T(4,128)(2,1)} %constant_dynamic-update-slice_fusion.11, bf16[1,4,12,128]{3,1,2,0:T(4,128)(2,1)S(1)} %stack.40), kind=kLoop, calls=%fused_computation.12 | loop fusion | bytes 24576
  5.7 0.6 %constant_dynamic-update-slice_fusion.9 = bf16[16,4,12,128]{3,1,2,0:T(4,128)(2,1)} fusion(bf16[16,4,12,128]{3,1,2,0:T(4,128)(2,1)} %constant_dynamic-update-slice_fusion.10, bf16[1,4,12,128]{3,1,2,0:T(4,128)(2,1)S(1)} %stack.41), kind=kLoop, calls=%fused_computation.11 | loop fusion | bytes 24576
  6.4 0.6 %constant_dynamic-update-slice_fusion.8 = bf16[16,4,12,128]{3,1,2,0:T(4,128)(2,1)} fusion(bf16[16,4,12,128]{3,1,2,0:T(4,128)(2,1)} %constant_dynamic-update-slice_fusion.9, bf16[1,4,12,128]{3,1,2,0:T(4,128)(2,1)S(1)} %stack.42), kind=kLoop, calls=%fused_computation.10 | loop fusion | bytes 24576
  7.0 0.6 %constant_dynamic-update-slice_fusion.7 = bf16[16,4,12,128]{3,1,2,0:T(4,128)(2,1)} fusion(bf16[16,4,12,128]{3,1,2,0:T(4,128)(2,1)} %constant_dynamic-update-slice_fusion.8, bf16[1,4,12,128]{3,1,2,0:T(4,128)(2,1)S(1)} %stack.35), kind=kLoop, calls=%fused_computation.9 | loop fusion | bytes 24576
  7.6 0.6 %constant_dynamic-update-slice_fusion.6 = bf16[16,4,12,128]{3,1,2,0:T(4,128)(2,1)} fusion(bf16[16,4,12,128]{3,1,2,0:T(4,128)(2,1)} %constant_dynamic-update-slice_fusion.7, bf16[1,4,12,128]{3,1,2,0:T(4,128)(2,1)S(1)} %stack.36), kind=kLoop, calls=%fused_computation.8 | loop fusion | bytes 24576
  8.2 0.6 %constant_dynamic-update-slice_fusion.5 = bf16[16,4,12,128]{3,1,2,0:T(4,128)(2,1)} fusion(bf16[16,4,12,128]{3,1,2,0:T(4,128)(2,1)} %constant_dynamic-update-slice_fusion.6, bf16[16,12,128]{2,0,1:T(8,128)(2,1)S(1)} %reshape.32), kind=kLoop, calls=%fused_computation.7 | loop fusion | bytes 61440
  8.8 0.6 %constant_dynamic-update-slice_fusion.4 = bf16[16,4,12,128]{3,1,2,0:T(4,128)(2,1)} fusion(bf16[16,4,12,128]{3,1,2,0:T(4,128)(2,1)} %constant_dynamic-update-slice_fusion.5, bf16[16,12,128]{2,0,1:T(8,128)(2,1)S(1)} %reshape.32), kind=kLoop, calls=%fused_computation.6 | loop fusion | bytes 61440
  9.4 0.6 %constant_dynamic-update-slice_fusion.3 = bf16[16,4,12,128]{3,1,2,0:T(4,128)(2,1)} fusion(bf16[16,4,12,128]{3,1,2,0:T(4,128)(2,1)} %constant_dynamic-update-slice_fusion.4, bf16[1,4,12,128]{3,1,2,0:T(4,128)(2,1)S(1)} %stack.39), kind=kLoop, calls=%fused_computation.5 | loop fusion | bytes 24576
  10.0 0.6 %constant_dynamic-update-slice_fusion.2 = bf16[16,4,12,128]{3,1,2,0:T(4,128)(2,1)} fusion(bf16[16,4,12,128]{3,1,2,0:T(4,128)(2,1)} %constant_dynamic-update-slice_fusion.3, bf16[1,4,12,128]{3,1,2,0:T(4,128)(2,1)S(1)} %stack.40), kind=kLoop, calls=%fused_computation.4 | loop fusion | bytes 24576
  11.2 0.6 %constant_dynamic-update-slice_fusion = bf16[16,4,12,128]{3,1,2,0:T(4,128)(2,1)} fusion(bf16[16,4,12,128]{3,1,2,0:T(4,128)(2,1)} %constant_dynamic-update-slice_fusion.1, bf16[1,4,12,128]{3,1,2,0:T(4,128)(2,1)S(1)} %stack.42), kind=kLoop, calls=%fused_computation.2 | loop fusion | bytes 24576 | tf_op jit(solution)/shard_map/stack | solution.py:225
  11.8 7.4 %all-to-all-start = ((bf16[16,4,12,128]{3,1,2,0:T(4,128)(2,1)}), bf16[16,4,12,128]{3,1,2,0:T(4,128)(2,1)S(1)}, u32[]{:S(2)}, u32[]{:S(2)}) async-start(bf16[16,4,12,128]{3,1,2,0:T(4,128)(2,1)} %constant_dynamic-update-slice_fusion), calls=%async_computation | async-start | bytes 393216 | tf_op jit(solution)/shard_map/all_to_all | solution.py:226
  19.2 1.2 %reshape.34.fg_ref = f32[1,384]{1,0:T(1,128)} reshape(f32[384]{0:T(512)} %param.10) | data formatting | bytes 3072 | tf_op jit(solution)/shard_map/reshape | solution.py:253
  20.5 1.3 %reshape.35.hg_ref = f32[1,384]{1,0:T(1,128)} reshape(f32[384]{0:T(512)} %param.12) | data formatting | bytes 3072 | tf_op jit(solution)/shard_map/reshape | solution.py:255
  21.7 0.9 %copy.26 = bf16[384,48]{1,0:T(8,128)(2,1)S(1)} copy(bf16[384,48]{0,1:T(8,128)(2,1)} %param.13) | data formatting | bytes 73728 | tf_op args[6]
  22.6 0.7 %pad.9.hw_ref = bf16[384,128]{1,0:T(8,128)(2,1)} pad(bf16[384,48]{1,0:T(8,128)(2,1)S(1)} %copy.26, bf16[]{:T(256)} %constant.6.clone.1), padding=0_0x0_80 | pad | bytes 135170 | tf_op jit(solution)/shard_map/jit(_pad)/pad | solution.py:256
  23.3 4.9 %all-to-all-done = bf16[16,4,12,128]{3,1,2,0:T(4,128)(2,1)S(1)} async-done(((bf16[16,4,12,128]{3,1,2,0:T(4,128)(2,1)}), bf16[16,4,12,128]{3,1,2,0:T(4,128)(2,1)S(1)}, u32[]{:S(2)}, u32[]{:S(2)}) %all-to-all-start) | async-done | bytes 196640 | tf_op jit(solution)/shard_map/all_to_all | solution.py:226
  28.2 0.7 %copy.27.recv_ref = bf16[16,4,12,128]{3,2,1,0:T(8,128)(2,1)} copy(bf16[16,4,12,128]{3,1,2,0:T(4,128)(2,1)S(1)} %all-to-all-done) | data formatting | bytes 393216 | tf_op jit(solution)/shard_map/all_to_all | solution.py:226
  28.9 26.2 %shard_map.73 = f32[1,2,3,48,128]{4,3,2,1,0:T(8,128)} custom-call(s32[1]{0:T(128)} %bitcast.place_ref, s32[4]{0:T(128)} %clip_ref.1, bf16[16,4,12,128]{3,2,1,0:T(8,128)(2,1)} %copy.27.recv_ref, bf16[9,48,384]{2,1,0:T(8,128)(2,1)} %bitcast.47, f32[1,384]{1,0:T(1,128)} %reshape.34.fg_ref, bf16[3,3,3,384,384]{4,3,2,1,0:T(8,128)(2,1)} %mc_ref.1, ...), custom_call_target="tpu_custom_call" | custom-call | tf_op jit(solution)/shard_map/pallas_call | solution.py:248
  (9 shorter events, 1.7 us)
Async XLA Ops:
  11.8 16.4 %all-to-all-start = ((bf16[16,4,12,128]{3,1,2,0:T(4,128)(2,1)}), bf16[16,4,12,128]{3,1,2,0:T(4,128)(2,1)S(1)}, u32[]{:S(2)}, u32[]{:S(2)}) async-start(bf16[16,4,12,128]{3,1,2,0:T(4,128)(2,1)} %constant_dynamic-update-slice_fusion), calls=%async_computation | async-start | bytes 393216 | tf_op jit(solution)/shard_map/all_to_all | solution.py:226

commit v2 on v1

--- a/solution.py
+++ b/solution.py
@@ -208,6 +208,12 @@
             out_ref[0, t, colour] = sums[0] + sums[1]
 
 
+def window_kernel(tiles, packed_ref, out_ref):
+    for dest in range(tiles):
+        strip = (dest - (STRIPS // 2 - 1)) % tiles % STRIPS
+        out_ref[dest] = packed_ref[2 * strip : 2 * strip + TILES_WIN]
+
+
 def per_device(latents, clip_index, first_conv, first_gain, middle_conv, head_gain, head_weight):
     tiles = lax.axis_size("tile")
     place = lax.axis_index("tile").astype(jnp.int32).reshape(1)
@@ -218,11 +224,13 @@
     packed = latents.reshape(rows, CLAT, width // PER_TILE, PER_TILE).transpose(2, 0, 3, 1)
     packed = packed.reshape(width // PER_TILE, rows, LANE)
     packed = jnp.pad(packed, ((1, 1), (0, 0), (0, 0)))
-    sent = []
-    for dest in range(tiles):
-        strip = (dest - (STRIPS // 2 - 1)) % tiles % STRIPS
-        sent.append(packed[2 * strip : 2 * strip + TILES_WIN])
-    sent = jnp.stack(sent)
+    sent = pl.pallas_call(
+        functools.partial(window_kernel, tiles),
+        out_shape=jax.ShapeDtypeStruct((tiles, TILES_WIN, rows, LANE), packed.dtype),
+        in_specs=[pl.BlockSpec(memory_space=pltpu.VMEM)],
+        out_specs=pl.BlockSpec(memory_space=pltpu.VMEM),
+        compiler_params=pltpu.CompilerParams(vmem_limit_bytes=8 * 1024 * 1024),
+    )(packed)
     came = lax.all_to_all(sent, "tile", 0, 0, tiled=True)
 
     vmem = pl.BlockSpec(memory_space=pltpu.VMEM)

time: 55.5 us -> 45.9 us (0.83)
  local copies, waits for them, and re-layouts: 16.6 us -> 6.87 us
    unnamed x17 -> x2, local copies, waits for them, and re-layouts: 11 us -> 1.91 us
    another operation x7 -> x0, local copies, waits for them, and re-layouts: 1.33 us -> none  [per_device(): sent = jnp.stack(sent)]
    pallas_call x0 -> x1, local copies, waits for them, and re-layouts: none -> 0.74 us  [per_device(): pl.pallas_call(functools.partial(window_kernel, tiles), out_shape=jax.Sha...]
  transfers between devices with their start and end apart: 1 -> 1, of which waited for: 1 -> 1; matrix products, arithmetic and copies ran while one was open for 7% -> 9% of each run, Pallas kernels for 0% -> 0%
where the time goes in v2:
time: 45.9 us; the launch traced here: 45.5 us
  Pallas kernels  26.3 us (57%)
  starting transfers between devices  7.41 us (16%)
  local copies, waits for them, and re-layouts  6.87 us (15%)
  waiting for transfers between devices  4.89 us (11%)
    pallas_call x1, Pallas kernels, per_device(): call(place, clip_index, came, first_conv.reshape(9, 3 * CLAT, CH), first_...  26.2 us
    all_to_all x1, starting transfers between devices, per_device(): came = lax.all_to_all(sent, 'tile', 0, 0, tiled=True)  7.41 us
    all_to_all x1, waiting for transfers between devices, per_device(): came = lax.all_to_all(sent, 'tile', 0, 0, tiled=True)  4.89 us
    unnamed x2, local copies, waits for them, and re-layouts  1.91 us
    reshape x1, local copies, waits for them, and re-layouts, per_device(): first_gain.reshape(1, CH)  1.26 us
    reshape x1, local copies, waits for them, and re-layouts, per_device(): head_gain.reshape(1, CH)  1.24 us
  transfers between devices with their start and end apart: 1, of which 1 were waited for; matrix products, arithmetic and copies ran while one was open for 9% of the time, Pallas kernels for 0%

profile of v2, /device:TPU:0, one launch (start us, length us, event | category | flops | bytes accessed | tf_op | source)
XLA Modules:
  0.0 45.5 jit_solution(12064258353468634561)
XLA Ops:
  0.0 1.0 %copy.13 = bf16[12,16,128]{1,2,0:T(8,128)(2,1)S(1)} copy(bf16[12,16,128]{2,1,0:T(8,128)(2,1)} %param.7) | data formatting | bytes 98304 | tf_op args[0]
  1.0 0.3 reshape.20
  1.4 0.7 %copy.15 = bf16[16,4,12,128]{3,1,2,0:T(4,128)(2,1)} copy(bf16[16,4,12,128]{3,2,1,0:T(8,128)(2,1)S(1)} %shard_map.73) | data formatting | bytes 393216 | tf_op jit(solution)/shard_map/pallas_call | solution.py:227
  2.1 7.4 %all-to-all-start = ((bf16[16,4,12,128]{3,1,2,0:T(4,128)(2,1)}), bf16[16,4,12,128]{3,1,2,0:T(4,128)(2,1)S(1)}, u32[]{:S(2)}, u32[]{:S(2)}) async-start(bf16[16,4,12,128]{3,1,2,0:T(4,128)(2,1)} %copy.15), calls=%async_computation | async-start | bytes 393216 | tf_op jit(solution)/shard_map/all_to_all | solution.py:234
  9.6 0.9 %copy.16 = bf16[384,48]{1,0:T(8,128)(2,1)S(1)} copy(bf16[384,48]{0,1:T(8,128)(2,1)} %param.13) | data formatting | bytes 73728 | tf_op args[6]
  10.4 0.7 %pad.9.hw_ref = bf16[384,128]{1,0:T(8,128)(2,1)} pad(bf16[384,48]{1,0:T(8,128)(2,1)S(1)} %copy.16, bf16[]{:T(256)} %constant.6.clone.1), padding=0_0x0_80 | pad | bytes 135170 | tf_op jit(solution)/shard_map/jit(_pad)/pad | solution.py:264
  11.1 1.3 %reshape.22.fg_ref = f32[1,384]{1,0:T(1,128)} reshape(f32[384]{0:T(512)} %param.10) | data formatting | bytes 3072 | tf_op jit(solution)/shard_map/reshape | solution.py:261
  12.4 1.2 %reshape.23.hg_ref = f32[1,384]{1,0:T(1,128)} reshape(f32[384]{0:T(512)} %param.12) | data formatting | bytes 3072 | tf_op jit(solution)/shard_map/reshape | solution.py:263
  13.6 4.9 %all-to-all-done = bf16[16,4,12,128]{3,1,2,0:T(4,128)(2,1)S(1)} async-done(((bf16[16,4,12,128]{3,1,2,0:T(4,128)(2,1)}), bf16[16,4,12,128]{3,1,2,0:T(4,128)(2,1)S(1)}, u32[]{:S(2)}, u32[]{:S(2)}) %all-to-all-start) | async-done | bytes 196640 | tf_op jit(solution)/shard_map/all_to_all | solution.py:234
  18.5 0.8 %copy.17.recv_ref = bf16[16,4,12,128]{3,2,1,0:T(8,128)(2,1)} copy(bf16[16,4,12,128]{3,1,2,0:T(4,128)(2,1)S(1)} %all-to-all-done) | data formatting | bytes 393216 | tf_op jit(solution)/shard_map/all_to_all | solution.py:234
  19.3 26.2 %shard_map.74 = f32[1,2,3,48,128]{4,3,2,1,0:T(8,128)} custom-call(s32[1]{0:T(128)} %bitcast.place_ref, s32[4]{0:T(128)} %clip_ref.1, bf16[16,4,12,128]{3,2,1,0:T(8,128)(2,1)} %copy.17.recv_ref, bf16[9,48,384]{2,1,0:T(8,128)(2,1)} %bitcast.10, f32[1,384]{1,0:T(1,128)} %reshape.22.fg_ref, bf16[3,3,3,384,384]{4,3,2,1,0:T(8,128)(2,1)} %mc_ref.1, ...), custom_call_target="tpu_custom_call" | custom-call | tf_op jit(solution)/shard_map/pallas_call | solution.py:256
  (3 shorter events, 0.1 us)
Async XLA Ops:
  2.1 16.4 %all-to-all-start = ((bf16[16,4,12,128]{3,1,2,0:T(4,128)(2,1)}), bf16[16,4,12,128]{3,1,2,0:T(4,128)(2,1)S(1)}, u32[]{:S(2)}, u32[]{:S(2)}) async-start(bf16[16,4,12,128]{3,1,2,0:T(4,128)(2,1)} %copy.15), calls=%async_computation | async-start | bytes 393216 | tf_op jit(solution)/shard_map/all_to_all | solution.py:234
